TPU v7x, 32 devices: a whole 2x2x4 slice. The times are simulated.
32 devices in a mesh: grp: 2 (over x), leaf: 16 (over z, y, core).
Axes of the slice: x: 2, y: 2, z: 4, core: 2. Of those that a mesh axis runs over, the one named last changes fastest.
Arguments:
- snapshots: float32 [131072, 256], P(('grp', 'leaf')), may hold values from -150 to 150
- sketch: float32 [256, 64], replicated, may hold values from -6 to 6
Outputs:
- recon: bfloat16 [131072, 256], P(('grp', 'leaf'))
All inputs are finite; a program needn't handle non-finite values.
Results may differ from a plain program's by a relative error of at most 0.001.
Values sent between devices are 32-bit elements; how exact they have to be, the bound alone decides.
A program may use at most 64 MiB of HBM per device.

v0:
```python
import jax
import jax.numpy as jnp
from jax import lax
from jax.sharding import PartitionSpec as P

highest_precision = lax.Precision.HIGHEST


def orthonormal(candidate):
    for repeat_index in range(2):
        correlation = jnp.dot(candidate.T, candidate, precision=highest_precision)
        lower_factor = jnp.linalg.cholesky(correlation)
        candidate = jax.scipy.linalg.solve_triangular(lower_factor, candidate.T, lower=True).T
    return candidate


def subspace(gram_sum, sketch):
    mode_basis = orthonormal(jnp.dot(gram_sum, sketch, precision=highest_precision))
    return mode_basis


def factor(gram_sum, sketch):
    mode_basis = subspace(gram_sum, sketch)
    reduced = jnp.dot(
        mode_basis.T,
        jnp.dot(gram_sum, mode_basis, precision=highest_precision),
        precision=highest_precision,
    )
    reduced = 0.5 * (reduced + reduced.T)
    lower_factor = jnp.linalg.cholesky(reduced)
    return jnp.dot(lower_factor.T, mode_basis.T, precision=highest_precision)


def add_square(block_rows):
    return jnp.dot(block_rows.T, block_rows, precision=highest_precision)


def local(snapshots, sketch):
    local_gram = jnp.dot(
        snapshots.T, snapshots, precision=highest_precision, preferred_element_type=jnp.float32
    )
    first_factor = factor(local_gram, sketch)
    group_gram = add_square(lax.all_gather(first_factor, "grp", axis=0, tiled=True))
    second_factor = factor(group_gram, sketch)
    total_gram = add_square(lax.all_gather(second_factor, "leaf", axis=0, tiled=True))
    mode_basis = subspace(total_gram, sketch)
    projector = jnp.dot(mode_basis, mode_basis.T, precision=highest_precision)
    return jnp.dot(snapshots, projector, precision=highest_precision).astype(jnp.bfloat16)


def solution(mesh):
    return jax.shard_map(
        local,
        mesh=mesh,
        in_specs=(P(("grp", "leaf"), None), P()),
        out_specs=P(("grp", "leaf"), None),
        check_vma=False,
    )
```

profile of v0, /device:TPU:0, one launch (start us, length us, event | category | flops | bytes accessed | tf_op | source)
XLA Modules:
  0.0 181.6 jit_solution(13125589537774815107)
XLA Ops:
  6.5 9.9 %fusion.64 = f32[256,256]{1,0:T(8,128)S(1)} fusion(f32[4096,256]{1,0:T(8,128)} %param.5), kind=kOutput, calls=%fused_computation.90 | convolution fusion | flops 3221225472 | bytes 4456448 | tf_op jit(solution)/shard_map/dot_general | solution.py:39
  16.5 0.4 fusion.65
  17.1 5.8 %cholesky.134 = f32[64,64]{1,0:T(8,128)S(1)} custom-call(f32[64,64]{1,0:T(8,128)S(1)} %fusion.31), custom_call_target="Cholesky" | custom-call | tf_op jit(solution)/shard_map/jit(cholesky)/cholesky | solution.py:12
  23.0 0.6 compare_reduce_fusion.7
  23.7 0.7 fusion.7
  24.3 4.9 %custom-call.10 = f32[1,64,64]{1,2,0:T(8,128)S(1)} custom-call(f32[1,64,64]{2,1,0:T(8,128)S(1)} %fusion.7), custom_call_target="InvertDiagBlocksLowerTriangular" | custom-call | tf_op jit(solution)/shard_map/jit(_solve_triangular)/triangular_solve | solution.py:13
  29.2 0.3 fusion.5
  29.8 5.8 %cholesky.145 = f32[64,64]{1,0:T(8,128)S(1)} custom-call(f32[64,64]{1,0:T(8,128)S(1)} %fusion.29), custom_call_target="Cholesky" | custom-call | tf_op jit(solution)/shard_map/jit(cholesky)/cholesky | solution.py:12
  35.7 0.6 compare_reduce_fusion.6
  36.3 0.7 fusion.8
  37.0 4.9 %custom-call.11 = f32[1,64,64]{1,2,0:T(8,128)S(1)} custom-call(f32[1,64,64]{2,1,0:T(8,128)S(1)} %fusion.8), custom_call_target="InvertDiagBlocksLowerTriangular" | custom-call | tf_op jit(solution)/shard_map/jit(_solve_triangular)/triangular_solve | solution.py:13
  41.9 0.3 fusion.27
  42.2 0.4 fusion.68
  42.9 5.8 %cholesky.156 = f32[64,64]{1,0:T(8,128)S(1)} custom-call(f32[64,64]{1,0:T(8,128)S(1)} %fusion.25), custom_call_target="Cholesky" | custom-call | tf_op jit(solution)/shard_map/jit(cholesky)/cholesky | solution.py:30
  48.8 0.6 compare_reduce_fusion.5
  49.5 0.9 fusion.36
  50.4 6.0 %all_gather.6 = f32[128,256]{1,0:T(8,128)S(1)} all-gather(f32[64,256]{1,0:T(8,128)S(1)} %fusion.36), channel_id=1, replica_groups=mesh['grp'=2,'leaf'=16] {'grp'}, dimensions={0}, use_global_device_ids=true | all-gather | bytes 196608 | tf_op jit(solution)/shard_map/all_gather | solution.py:43
  56.4 0.4 fusion.70
  56.8 0.4 fusion.71
  57.5 5.8 %cholesky.167 = f32[64,64]{1,0:T(8,128)S(1)} custom-call(f32[64,64]{1,0:T(8,128)S(1)} %fusion.24), custom_call_target="Cholesky" | custom-call | tf_op jit(solution)/shard_map/jit(cholesky)/cholesky | solution.py:12
  63.4 0.6 compare_reduce_fusion.4
  64.1 0.7 fusion.9
  64.7 4.9 %custom-call.12 = f32[1,64,64]{1,2,0:T(8,128)S(1)} custom-call(f32[1,64,64]{2,1,0:T(8,128)S(1)} %fusion.9), custom_call_target="InvertDiagBlocksLowerTriangular" | custom-call | tf_op jit(solution)/shard_map/jit(_solve_triangular)/triangular_solve | solution.py:13
  69.6 0.3 fusion.3
  70.2 5.8 %cholesky.178 = f32[64,64]{1,0:T(8,128)S(1)} custom-call(f32[64,64]{1,0:T(8,128)S(1)} %fusion.22), custom_call_target="Cholesky" | custom-call | tf_op jit(solution)/shard_map/jit(cholesky)/cholesky | solution.py:12
  76.1 0.6 compare_reduce_fusion.3
  76.7 0.7 fusion.10
  77.4 4.9 %custom-call.13 = f32[1,64,64]{1,2,0:T(8,128)S(1)} custom-call(f32[1,64,64]{2,1,0:T(8,128)S(1)} %fusion.10), custom_call_target="InvertDiagBlocksLowerTriangular" | custom-call | tf_op jit(solution)/shard_map/jit(_solve_triangular)/triangular_solve | solution.py:13
  82.3 0.3 fusion.20
  82.6 0.4 fusion.74
  83.3 5.8 %cholesky.189 = f32[64,64]{1,0:T(8,128)S(1)} custom-call(f32[64,64]{1,0:T(8,128)S(1)} %fusion.18), custom_call_target="Cholesky" | custom-call | tf_op jit(solution)/shard_map/jit(cholesky)/cholesky | solution.py:30
  89.2 0.7 compare_reduce_fusion.2
  89.9 1.6 fusion.34
  91.5 39.8 %all-gather.2.cloned.1.call-done = f32[1024,256]{1,0:T(8,128)} async-done(((f32[64,256]{1,0:T(8,128)}), f32[1024,256]{1,0:T(8,128)}) %all-gather.2.cloned.1.call-update) | async-done | bytes 1048592 | tf_op jit(solution)/shard_map/all_gather | solution.py:45
  131.3 3.4 %fusion.76 = f32[256,256]{1,0:T(8,128)S(1)} fusion(f32[1024,256]{1,0:T(8,128)} %all-gather.2.cloned.1.call-done), kind=kOutput, calls=%fused_computation.102 | convolution fusion | flops 805306368 | bytes 1310720 | tf_op jit(solution)/shard_map/dot_general | solution.py:35
  134.7 0.4 fusion.77
  135.4 5.8 %cholesky.200 = f32[64,64]{1,0:T(8,128)S(1)} custom-call(f32[64,64]{1,0:T(8,128)S(1)} %fusion.17), custom_call_target="Cholesky" | custom-call | tf_op jit(solution)/shard_map/jit(cholesky)/cholesky | solution.py:12
  141.3 0.6 compare_reduce_fusion.1
  141.9 0.7 fusion.11
  142.6 4.9 %custom-call.14 = f32[1,64,64]{1,2,0:T(8,128)S(1)} custom-call(f32[1,64,64]{2,1,0:T(8,128)S(1)} %fusion.11), custom_call_target="InvertDiagBlocksLowerTriangular" | custom-call | tf_op jit(solution)/shard_map/jit(_solve_triangular)/triangular_solve | solution.py:13
  147.5 0.3 fusion.1
  148.1 5.8 %cholesky.211 = f32[64,64]{1,0:T(8,128)S(1)} custom-call(f32[64,64]{1,0:T(8,128)S(1)} %fusion.15), custom_call_target="Cholesky" | custom-call | tf_op jit(solution)/shard_map/jit(cholesky)/cholesky | solution.py:12
  153.9 0.6 compare_reduce_fusion
  154.6 0.7 fusion.12
  155.2 5.0 %custom-call.15 = f32[1,64,64]{1,2,0:T(8,128)S(1)} custom-call(f32[1,64,64]{2,1,0:T(8,128)S(1)} %fusion.12), custom_call_target="InvertDiagBlocksLowerTriangular" | custom-call | tf_op jit(solution)/shard_map/jit(_solve_triangular)/triangular_solve | solution.py:13
  160.5 0.4 fusion.80
  160.9 11.3 %fusion = bf16[4096,256]{0,1:T(8,128)(2,1)S(1)} fusion(f32[256,256]{1,0:T(8,128)S(1)} %fusion.80, f32[4096,256]{1,0:T(8,128)} %param.5), kind=kOutput, calls=%fused_computation.1 | convolution fusion | flops 3222274048 | bytes 6553600 | tf_op jit(solution)/shard_map/dot_general | solution.py:48
  172.3 2.5 %copy.13 = bf16[4096,256]{1,0:T(8,128)(2,1)} copy(bf16[4096,256]{0,1:T(8,128)(2,1)S(1)} %fusion) | data formatting | bytes 4194304 | tf_op jit(solution)/shard_map/convert_element_type | solution.py:48
  (41 shorter events, 3.0 us)
Async XLA Ops:
  6.5 9.9 %copy-start = (f32[256,64]{0,1:T(8,128)S(1)}, f32[256,64]{0,1:T(8,128)}, u32[]{:S(2)}) copy-start(f32[256,64]{0,1:T(8,128)} %param.6) | copy-start | bytes 196612
  6.5 124.8 %all-gather.2.cloned.1.call-start = ((), (), s32[]{:S(2)}) async-start(), calls=%async_computation | async-start | bytes 1114112 | tf_op jit(solution)/shard_map/all_gather | solution.py:45
Sparse Core Ops, SparseCore 0:
  91.7 39.6 all-gather.1
where the time goes:
time: 182 us
  other arithmetic  85.7 us (47%)
  waiting for transfers between devices  39.8 us (22%)
  matrix products  33 us (18%)
  between operations  13.8 us (8%)
  blocking collectives  6.05 us (3%)
  local copies, waits for them, and re-layouts  3.2 us (2%)
    all_gather x1, waiting for transfers between devices, local(): lax.all_gather(second_factor, 'leaf', axis=0, tiled=True)  39.8 us
    another operation x18, other arithmetic, orthonormal(): lower_factor = jnp.linalg.cholesky(correlation)  39.1 us
    another operation x12, other arithmetic, orthonormal(): jax.scipy.linalg.solve_triangular(lower_factor, candidate.T, lower=True)  33.4 us
    another operation x6, other arithmetic, factor(): lower_factor = jnp.linalg.cholesky(reduced)  13.1 us
    dot_general x1, matrix products, local(): jnp.dot(snapshots, projector, precision=highest_precision)  11.3 us
    dot_general x1, matrix products, local(): jnp.dot(snapshots.T, snapshots, precision=highest_precision, preferred_el...  9.91 us
    all_gather x1, blocking collectives, local(): lax.all_gather(first_factor, 'grp', axis=0, tiled=True)  6.05 us
    dot_general x2, matrix products, add_square(): return jnp.dot(block_rows.T, block_rows, precision=highest_precision)  3.77 us
  transfers between devices with their start and end apart: 1, of which 1 were waited for; matrix products, arithmetic and copies ran while one was open for 0% of the time, Pallas kernels for 0%

commit v1 on v0

v1 whole, which is shorter than its diff:
```python
import functools

import jax
import jax.numpy as jnp
from jax import lax
from jax.experimental import pallas as pl
from jax.experimental.pallas import tpu as pltpu
from jax.sharding import PartitionSpec as P

MESH = pl.DeviceIdType.MESH
VMEM = pl.BlockSpec(memory_space=pltpu.VMEM)
LANES = 128
CHUNK = 512


def dot(a, b, ca=1, cb=0):
    return lax.dot_general(
        a, b, (((ca,), (cb,)), ((), ())),
        precision=lax.Precision.HIGHEST, preferred_element_type=jnp.float32,
    )


def fast(a, b, ca=1, cb=0):
    return lax.dot_general(a, b, (((ca,), (cb,)), ((), ())), preferred_element_type=jnp.float32)


def split(x):
    hi = x.astype(jnp.bfloat16)
    return hi, (x - hi.astype(jnp.float32)).astype(jnp.bfloat16)


def identity(n):
    return (lax.broadcasted_iota(jnp.int32, (n, n), 0) == lax.broadcasted_iota(jnp.int32, (n, n), 1)).astype(jnp.float32)


def inverse_factor(c, rows_ref):
    m = c.shape[0]
    full = jnp.concatenate([c, identity(m)], axis=1)
    width = 2 * m
    blocks = [full[8 * k : 8 * k + 8] for k in range(m // 8)]
    for j in range(0, m, 2):
        k, s = j // 8, j % 8
        lead = blocks[k]
        cols = [
            (
                jnp.broadcast_to(blocks[i][:, j : j + 1], (8, width)),
                jnp.broadcast_to(blocks[i][:, j + 1 : j + 2], (8, width)),
            )
            for i in range(k, m // 8)
        ]
        r0, r1 = lead[s : s + 1], lead[s + 1 : s + 2]
        a, b, d = cols[0][0][s : s + 1], cols[0][0][s + 1 : s + 2], cols[0][1][s + 1 : s + 2]
        det = a * d - b * b
        inv = 1.0 / det
        t0 = (d * r0 - b * r1) * inv
        t1 = (a * r1 - b * r0) * inv
        for i in range(k, m // 8):
            c0, c1 = cols[i - k]
            blocks[i] = blocks[i] - c0 * t0 - c1 * t1
        ia = lax.rsqrt(a)
        rows_ref[j : j + 1, :] = r0 * ia
        rows_ref[j + 1 : j + 2, :] = (a * r1 - b * r0) * (ia * lax.rsqrt(det))
    return rows_ref[:, m:]


def orthonormal(yt, rows_ref):
    m = yt.shape[0]
    qt = dot(inverse_factor(dot(yt, yt, 1, 1), rows_ref), yt)
    err = identity(m) - dot(qt, qt, 1, 1)
    fix = 0.5 * err + 0.375 * dot(err, err)
    return qt + dot(fix, qt)


def first_kernel(x_hbm, st_ref, qt_ref, h_ref, xbuf, acc, acc2, rows_ref, sems):
    chunks = x_hbm.shape[0] // CHUNK
    cols = x_hbm.shape[1]

    def copy(i):
        at = pl.ds(pl.multiple_of(i * CHUNK, CHUNK), CHUNK)
        return pltpu.make_async_copy(x_hbm.at[at], xbuf.at[at], sems.at[i])

    for i in range(chunks):
        copy(i).start()
    acc[...] = jnp.zeros_like(acc)
    acc2[...] = jnp.zeros_like(acc2)

    def step(i, carry):
        copy(i).wait()
        hi, mid = split(xbuf[pl.ds(pl.multiple_of(i * CHUNK, CHUNK), CHUNK), :])
        acc[...] += fast(hi, jnp.concatenate([hi, mid], axis=1), 0, 0)
        acc2[...] += fast(mid, mid, 0, 0)
        return carry

    lax.fori_loop(0, chunks, step, 0)
    cross = acc[:, cols:]
    acc2[...] = acc[:, :cols] + (cross + cross.T + acc2[...])
    gram = acc2[...]
    qt = orthonormal(dot(st_ref[...], gram), rows_ref)
    qt_ref[...] = qt
    h_ref[...] = dot(dot(qt, gram), qt, 1, 1)


def entry_barrier(axis_counts):
    barrier = pltpu.get_barrier_semaphore()
    total = 0
    for axis, n in axis_counts:
        me = lax.axis_index(axis)
        for d in range(1, n):
            pl.semaphore_signal(barrier, inc=1, device_id={axis: lax.rem(me + d, n)}, device_id_type=MESH)
        total += n - 1
    pl.semaphore_wait(barrier, total)


def group_kernel(n, qt_ref, h_ref, qs_ref, hs_ref, qland, hland, qsend, qrecv, hsend, hrecv):
    entry_barrier([("grp", n)])
    me = lax.axis_index("grp")
    copies = []
    for d in range(1, n):
        peer = {"grp": lax.rem(me + d, n)}
        for src, land, ss, rs in ((qt_ref, qland, qsend, qrecv), (h_ref, hland, hsend, hrecv)):
            copies.append(
                pltpu.make_async_remote_copy(
                    src_ref=src, dst_ref=land.at[d - 1], send_sem=ss.at[d - 1], recv_sem=rs.at[d - 1],
                    device_id=peer, device_id_type=MESH,
                )
            )
            copies[-1].start()
    qs_ref[0] = qt_ref[...]
    hs_ref[0] = h_ref[...]
    for copy in copies:
        copy.wait()
    for d in range(1, n):
        qs_ref[d] = qland[d - 1]
        hs_ref[d] = hland[d - 1]


def second_kernel(n, qs_ref, hs_ref, st_ref, zt_ref, rows_ref):
    st = st_ref[...]
    m, cols = st.shape
    qs = qs_ref[...].reshape(n * m, cols)
    us = dot(st, qs, 1, 1)
    vs = jnp.concatenate([dot(us[:, g * m : g * m + m], hs_ref[g]) for g in range(n)], axis=1)
    q2 = orthonormal(dot(vs, qs), rows_ref)
    u = dot(st, q2, 1, 1)
    s = dot(q2, qs, 1, 1)
    w = dot(u, s)
    w = jnp.concatenate([dot(w[:, g * m : g * m + m], hs_ref[g]) for g in range(n)], axis=1)
    zt_ref[...] = dot(dot(w, s, 1, 1), q2)


def sum_kernel(n, z_ref, y_ref, mine, land, reduced, gathered, rs_send, rs_recv, ag_send, ag_recv):
    entry_barrier([("leaf", n)])
    me = lax.axis_index("leaf")

    def exchange(d, source, target, ss, rs):
        peer = lax.rem(me + d, n)
        return pltpu.make_async_remote_copy(
            src_ref=source(peer), dst_ref=target.at[d - 1], send_sem=ss.at[d - 1], recv_sem=rs.at[d - 1],
            device_id={"leaf": peer}, device_id_type=MESH,
        )

    scatter = [exchange(d, lambda p: z_ref.at[p], land, rs_send, rs_recv) for d in range(1, n)]
    for copy in scatter:
        copy.start()
    total = z_ref[me]
    for d, copy in enumerate(scatter):
        copy.wait_recv()
        total = total + land[d]
    reduced[...] = total
    gather = [exchange(d, lambda p: reduced, gathered, ag_send, ag_recv) for d in range(1, n)]
    for copy in gather:
        copy.start()
    y_ref[me] = total
    for copy in scatter:
        copy.wait_send()
    for d in range(1, n):
        gather[d - 1].wait()
        y_ref[lax.rem(me + n - d, n)] = gathered[d - 1]


def project_kernel(x_hbm, yt_ref, o_hbm, xbuf, obuf, phi, pmid, rows_ref, sems, osems):
    chunks = x_hbm.shape[0] // CHUNK

    def copy(i):
        at = pl.ds(pl.multiple_of(i * CHUNK, CHUNK), CHUNK)
        return pltpu.make_async_copy(x_hbm.at[at], xbuf.at[at], sems.at[i])

    def out(i):
        at = pl.ds(pl.multiple_of(i * CHUNK, CHUNK), CHUNK)
        return pltpu.make_async_copy(obuf.at[at], o_hbm.at[at], osems.at[i])

    for i in range(chunks):
        copy(i).start()
    qt = orthonormal(yt_ref[...], rows_ref)
    hi, mid = split(dot(qt, qt, 0, 0))
    phi[...] = hi
    pmid[...] = mid

    def step(i, carry):
        copy(i).wait()
        at = pl.ds(pl.multiple_of(i * CHUNK, CHUNK), CHUNK)
        hi, mid = split(xbuf[at, :])
        obuf[at, :] = (fast(hi, phi[...]) + (fast(hi, pmid[...]) + fast(mid, phi[...]))).astype(jnp.bfloat16)
        out(i).start()
        return carry

    lax.fori_loop(0, chunks, step, 0)
    for i in range(chunks):
        out(i).wait()


def local(n_grp, n_leaf, x, sketch):
    rows, cols = x.shape
    modes = sketch.shape[1]
    chunks = rows // CHUNK
    f32 = jnp.float32
    hbm = pl.BlockSpec(memory_space=pl.ANY)
    st = sketch.T
    dma = pltpu.SemaphoreType.DMA
    qt, h = pl.pallas_call(
        first_kernel,
        out_shape=(jax.ShapeDtypeStruct((modes, cols), f32), jax.ShapeDtypeStruct((modes, modes), f32)),
        in_specs=[hbm, VMEM],
        out_specs=(VMEM, VMEM),
        scratch_shapes=[
            pltpu.VMEM((rows, cols), f32), pltpu.VMEM((cols, 2 * cols), f32), pltpu.VMEM((cols, cols), f32),
            pltpu.VMEM((modes, 2 * modes), f32), dma((chunks,)),
        ],
    )(x, st)
    qs, hs = pl.pallas_call(
        functools.partial(group_kernel, n_grp),
        out_shape=(jax.ShapeDtypeStruct((n_grp, modes, cols), f32), jax.ShapeDtypeStruct((n_grp, modes, modes), f32)),
        in_specs=[VMEM, VMEM],
        out_specs=(VMEM, VMEM),
        scratch_shapes=[
            pltpu.VMEM((n_grp - 1, modes, cols), f32), pltpu.VMEM((n_grp - 1, modes, modes), f32),
            dma((n_grp - 1,)), dma((n_grp - 1,)), dma((n_grp - 1,)), dma((n_grp - 1,)),
        ],
        compiler_params=pltpu.CompilerParams(collective_id=0, has_side_effects=True),
    )(qt, h)
    zt = pl.pallas_call(
        functools.partial(second_kernel, n_grp),
        out_shape=jax.ShapeDtypeStruct((modes, cols), f32),
        in_specs=[VMEM] * 3,
        out_specs=VMEM,
        scratch_shapes=[pltpu.VMEM((modes, 2 * modes), f32)],
    )(qs, hs, st)
    piece = (modes * cols // (n_leaf * LANES), LANES)
    wide = cols // LANES
    z = jnp.concatenate([zt[:, LANES * i : LANES * i + LANES] for i in range(wide)], axis=0).reshape(n_leaf, *piece)
    y = pl.pallas_call(
        functools.partial(sum_kernel, n_leaf),
        out_shape=jax.ShapeDtypeStruct((n_leaf, *piece), f32),
        in_specs=[VMEM],
        out_specs=VMEM,
        scratch_shapes=[
            pltpu.VMEM(piece, f32), pltpu.VMEM((n_leaf - 1, *piece), f32), pltpu.VMEM(piece, f32),
            pltpu.VMEM((n_leaf - 1, *piece), f32),
            dma((n_leaf - 1,)), dma((n_leaf - 1,)), dma((n_leaf - 1,)), dma((n_leaf - 1,)),
        ],
        compiler_params=pltpu.CompilerParams(collective_id=1, has_side_effects=True),
    )(z)
    y = y.reshape(wide * modes, LANES)
    yt = jnp.concatenate([y[modes * i : modes * i + modes] for i in range(wide)], axis=1)
    return pl.pallas_call(
        project_kernel,
        out_shape=jax.ShapeDtypeStruct((rows, cols), jnp.bfloat16),
        in_specs=[hbm, VMEM],
        out_specs=hbm,
        scratch_shapes=[
            pltpu.VMEM((rows, cols), f32), pltpu.VMEM((rows, cols), jnp.bfloat16),
            pltpu.VMEM((cols, cols), jnp.bfloat16), pltpu.VMEM((cols, cols), jnp.bfloat16),
            pltpu.VMEM((modes, 2 * modes), f32), dma((chunks,)), dma((chunks,)),
        ],
    )(x, yt)


def solution(mesh):
    return jax.shard_map(
        functools.partial(local, mesh.shape["grp"], mesh.shape["leaf"]),
        mesh=mesh,
        in_specs=(P(("grp", "leaf"), None), P()),
        out_specs=P(("grp", "leaf"), None),
        check_vma=False,
    )
```

time: 182 us -> 53.5 us (0.29)
  other arithmetic: 85.7 us -> 1.25 us
  Pallas kernels: 0 us -> 50.2 us
  waiting for transfers between devices: 39.8 us -> 0 us
  matrix products: 33 us -> 0 us
  between operations: 13.8 us -> 0.03 us
  blocking collectives: 6.05 us -> 0 us
    another operation x36 -> x0, other arithmetic: 85.6 us -> none  [the longest x18 39.1 us: orthonormal(): lower_factor = jnp.linalg.cholesky(correlation)]
    pallas_call x0 -> x5, Pallas kernels: none -> 50.2 us  [the longest x1 15.3 us: local(): pl.pallas_call(functools.partial(sum_kernel, n_leaf), out_shape=jax.Shape...]
    all_gather x1 -> x0, waiting for transfers between devices: 39.8 us -> none  [local(): lax.all_gather(second_factor, 'leaf', axis=0, tiled=True)]
    dot_general x20 -> x0, matrix products: 31.4 us -> none  [the longest x1 11.3 us: local(): jnp.dot(snapshots, projector, precision=highest_precision)]
    all_gather x1 -> x0, blocking collectives: 6.05 us -> none  [local(): lax.all_gather(first_factor, 'grp', axis=0, tiled=True)]
    convert_element_type x1 -> x0, local copies, waits for them, and re-layouts: 2.46 us -> none  [local(): jnp.dot(snapshots, projector, precision=highest_precision)]
  transfers between devices with their start and end apart: 1 -> 0, of which waited for: 1 -> 0; matrix products, arithmetic and copies ran while one was open for 0% -> 0% of each run, Pallas kernels for 0% -> 0%
where the time goes in v1:
time: 53.5 us; the launch traced here: 53 us
  Pallas kernels  50.2 us (94%)
  local copies, waits for them, and re-layouts  1.56 us (3%)
  other arithmetic  1.25 us (2%)
    pallas_call x1, Pallas kernels, local(): pl.pallas_call(functools.partial(sum_kernel, n_leaf), out_shape=jax.Shape...  15.3 us
    pallas_call x1, Pallas kernels, local(): pl.pallas_call(first_kernel, out_shape=(jax.ShapeDtypeStruct((modes, cols...  10.8 us
    pallas_call x1, Pallas kernels, local(): pl.pallas_call(project_kernel, out_shape=jax.ShapeDtypeStruct((rows, cols...  9.16 us
    pallas_call x1, Pallas kernels, local(): pl.pallas_call(functools.partial(second_kernel, n_grp), out_shape=jax.Sha...  7.61 us
    pallas_call x1, Pallas kernels, local(): pl.pallas_call(functools.partial(group_kernel, n_grp), out_shape=(jax.Sha...  7.32 us

profile of v1, /device:TPU:0, one launch (start us, length us, event | category | flops | bytes accessed | tf_op | source)
XLA Modules:
  0.0 53.0 jit_solution(17252043446053643961)
XLA Ops:
  0.0 10.8 %shard_map.28 = (f32[64,256]{1,0:T(8,128)}, f32[64,64]{1,0:T(8,128)}) custom-call(f32[4096,256]{1,0:T(8,128)} %x_hbm.3, f32[64,256]{1,0:T(8,128)} %bitcast.7), custom_call_target="tpu_custom_call" | custom-call | tf_op jit(solution)/shard_map/pallas_call | solution.py:220
  10.8 7.3 %shard_map.29 = (f32[2,64,256]{2,1,0:T(8,128)}, f32[2,64,64]{2,1,0:T(8,128)}) custom-call(f32[64,256]{1,0:T(8,128)} %get-tuple-element.9.qt_ref, f32[64,64]{1,0:T(8,128)} %get-tuple-element.10.h_ref), custom_call_target="tpu_custom_call" | custom-call | tf_op jit(solution)/shard_map/pallas_call | solution.py:230
  18.2 7.6 %shard_map.30 = f32[64,256]{1,0:T(8,128)} custom-call(f32[2,64,256]{2,1,0:T(8,128)} %get-tuple-element.11.qs_ref, f32[2,64,64]{2,1,0:T(8,128)} %get-tuple-element.12.hs_ref, f32[64,256]{1,0:T(8,128)} %bitcast.8), custom_call_target="tpu_custom_call" | custom-call | tf_op jit(solution)/shard_map/pallas_call | solution.py:241
  25.8 0.8 %fusion = (f32[64,128]{1,0:T(8,128)S(1)}, f32[64,128]{1,0:T(8,128)S(1)}) fusion(f32[64,256]{1,0:T(8,128)} %shard_map.30), kind=kLoop, calls=%fused_computation.4 | loop fusion | bytes 131072 | tf_op jit(solution)/shard_map/slice | solution.py:250
  26.5 0.6 %maximum_bitcast_fusion.z_ref = f32[16,8,128]{2,1,0:T(8,128)} fusion(f32[64,128]{1,0:T(8,128)S(1)} %get-tuple-element.16, f32[64,128]{1,0:T(8,128)S(1)} %get-tuple-element.15), kind=kLoop, calls=%fused_computation | loop fusion | flops 16384 | bytes 131072 | tf_op jit(solution)/shard_map/reshape | solution.py:250
  27.2 15.3 %shard_map.31 = f32[16,8,128]{2,1,0:T(8,128)} custom-call(f32[16,8,128]{2,1,0:T(8,128)} %maximum_bitcast_fusion.z_ref), custom_call_target="tpu_custom_call" | custom-call | tf_op jit(solution)/shard_map/pallas_call | solution.py:251
  42.5 0.8 %slice_bitcast_fusion.1 = (f32[64,128]{1,0:T(8,128)S(1)}, f32[64,128]{1,0:T(8,128)S(1)}) fusion(f32[16,8,128]{2,1,0:T(8,128)} %shard_map.31), kind=kLoop, calls=%fused_computation.3 | loop fusion | bytes 131072 | tf_op jit(solution)/shard_map/slice | solution.py:264
  43.3 0.6 %pad_maximum_fusion.yt_ref = f32[64,256]{1,0:T(8,128)} fusion(f32[64,128]{1,0:T(8,128)S(1)} %get-tuple-element.14, f32[64,128]{1,0:T(8,128)S(1)} %get-tuple-element.13), kind=kLoop, calls=%fused_computation.1 | loop fusion | flops 16384 | bytes 131072 | tf_op jit(solution)/shard_map/concatenate | solution.py:264
  43.9 9.2 %shard_map.32 = bf16[4096,256]{1,0:T(8,128)(2,1)} custom-call(f32[4096,256]{1,0:T(8,128)} %x_hbm.3, f32[64,256]{1,0:T(8,128)} %pad_maximum_fusion.yt_ref), custom_call_target="tpu_custom_call" | custom-call | tf_op jit(solution)/shard_map/pallas_call | solution.py:265

commit v2 on v1

v2 whole, which is shorter than its diff:
```python
import functools

import jax
import jax.numpy as jnp
from jax import lax
from jax.experimental import pallas as pl
from jax.experimental.pallas import tpu as pltpu
from jax.sharding import PartitionSpec as P

MESH = pl.DeviceIdType.MESH
VMEM = pl.BlockSpec(memory_space=pltpu.VMEM)
LANES = 128
CHUNK = 512


def dot(a, b, ca=1, cb=0):
    return lax.dot_general(
        a, b, (((ca,), (cb,)), ((), ())),
        precision=lax.Precision.HIGHEST, preferred_element_type=jnp.float32,
    )


def fast(a, b, ca=1, cb=0):
    return lax.dot_general(a, b, (((ca,), (cb,)), ((), ())), preferred_element_type=jnp.float32)


def split(x):
    hi = x.astype(jnp.bfloat16)
    return hi, (x - hi.astype(jnp.float32)).astype(jnp.bfloat16)


def three(a, b):
    (ah, am), (bh, bm) = split(a), split(b)
    return fast(ah, bh) + (fast(ah, bm) + fast(am, bh))


def identity(n):
    return (lax.broadcasted_iota(jnp.int32, (n, n), 0) == lax.broadcasted_iota(jnp.int32, (n, n), 1)).astype(jnp.float32)


def inverse_factor(c, rows_ref):
    m = c.shape[0]
    full = jnp.concatenate([c, identity(m)], axis=1)
    width = 2 * m
    blocks = [full[8 * k : 8 * k + 8] for k in range(m // 8)]
    for j in range(0, m, 2):
        k, s = j // 8, j % 8
        lead = blocks[k]
        cols = [
            (
                jnp.broadcast_to(blocks[i][:, j : j + 1], (8, width)),
                jnp.broadcast_to(blocks[i][:, j + 1 : j + 2], (8, width)),
            )
            for i in range(k, m // 8)
        ]
        r0, r1 = lead[s : s + 1], lead[s + 1 : s + 2]
        a, b, d = cols[0][0][s : s + 1], cols[0][0][s + 1 : s + 2], cols[0][1][s + 1 : s + 2]
        det = a * d - b * b
        inv = 1.0 / det
        t0 = (d * r0 - b * r1) * inv
        t1 = (a * r1 - b * r0) * inv
        for i in range(k, m // 8):
            c0, c1 = cols[i - k]
            blocks[i] = blocks[i] - c0 * t0 - c1 * t1
        ia = lax.rsqrt(a)
        rows_ref[j : j + 1, :] = r0 * ia
        rows_ref[j + 1 : j + 2, :] = (a * r1 - b * r0) * (ia * lax.rsqrt(det))
    return rows_ref[:, m:]


def orthonormal(yt, rows_ref):
    m = yt.shape[0]
    qt = dot(inverse_factor(dot(yt, yt, 1, 1), rows_ref), yt)
    err = identity(m) - dot(qt, qt, 1, 1)
    near = err.astype(jnp.bfloat16)
    fix = 0.5 * err + 0.375 * fast(near, near)
    return qt + three(fix, qt)


def merge_kernel(n_grp, n_leaf, x_hbm, st_ref, yt_ref, xbuf, acc, acc2, rows_ref, qall, hall, z, land, total, yall, sems, qsem, hsem, rsem, gsem):
    chunks = x_hbm.shape[0] // CHUNK
    m, cols = st_ref.shape
    grp, leaf = lax.axis_index("grp"), lax.axis_index("leaf")

    def copy(i):
        at = pl.ds(pl.multiple_of(i * CHUNK, CHUNK), CHUNK)
        return pltpu.make_async_copy(x_hbm.at[at], xbuf.at[at], sems.at[i])

    for i in range(chunks):
        copy(i).start()
    barrier = pltpu.get_barrier_semaphore()
    for axis, me, n in (("grp", grp, n_grp), ("leaf", leaf, n_leaf)):
        for d in range(1, n):
            pl.semaphore_signal(barrier, inc=1, device_id={axis: lax.rem(me + d, n)}, device_id_type=MESH)

    acc[...] = jnp.zeros_like(acc)
    acc2[...] = jnp.zeros_like(acc2)

    def step(i, carry):
        copy(i).wait()
        hi, mid = split(xbuf[pl.ds(pl.multiple_of(i * CHUNK, CHUNK), CHUNK), :])
        acc[...] += fast(hi, jnp.concatenate([hi, mid], axis=1), 0, 0)
        acc2[...] += fast(mid, mid, 0, 0)
        return carry

    lax.fori_loop(0, chunks, step, 0)
    cross = acc[:, cols:]
    gram = acc[:, :cols] + (cross + cross.T + acc2[...])
    qt = orthonormal(dot(st_ref[...], gram), rows_ref)
    qall[0] = qt
    pl.semaphore_wait(barrier, n_grp + n_leaf - 2)

    def send(src, dst, sem, d, axis, me, n):
        return pltpu.make_async_remote_copy(
            src_ref=src, dst_ref=dst, send_sem=sem.at[0, d - 1], recv_sem=sem.at[1, d - 1],
            device_id={axis: lax.rem(me + d, n)}, device_id_type=MESH,
        )

    to_group = [send(qall.at[0], qall.at[d], qsem, d, "grp", grp, n_grp) for d in range(1, n_grp)]
    for c in to_group:
        c.start()
    hall[0] = dot(dot(qt, gram), qt, 1, 1)
    to_group_h = [send(hall.at[0], hall.at[d], hsem, d, "grp", grp, n_grp) for d in range(1, n_grp)]
    for c in to_group_h:
        c.start()
    for c in to_group:
        c.wait()
    st = st_ref[...]
    qs = qall[...].reshape(n_grp * m, cols)
    us = dot(st, qs, 1, 1)
    for c in to_group_h:
        c.wait()
    vs = jnp.concatenate([dot(us[:, g * m : g * m + m], hall[g]) for g in range(n_grp)], axis=1)
    q2 = orthonormal(dot(vs, qs), rows_ref)
    u = dot(st, q2, 1, 1)
    s = dot(q2, qs, 1, 1)
    w = dot(u, s)
    w = jnp.concatenate([dot(w[:, g * m : g * m + m], hall[g]) for g in range(n_grp)], axis=1)
    zt = dot(dot(w, s, 1, 1), q2)

    rows = z.shape[1]
    for p in range(n_leaf):
        at, wide = (p * rows) % m, (p * rows) // m * LANES
        z[p] = zt[at : at + rows, wide : wide + LANES]
    scatter = [send(z.at[lax.rem(leaf + d, n_leaf)], land.at[d - 1], rsem, d, "leaf", leaf, n_leaf) for d in range(1, n_leaf)]
    for c in scatter:
        c.start()
    part = z[leaf]
    for d, c in enumerate(scatter):
        c.wait_recv()
        part = part + land[d]
    total[...] = part
    gather = [send(total, yall.at[leaf], gsem, d, "leaf", leaf, n_leaf) for d in range(1, n_leaf)]
    for c in gather:
        c.start()
    yall[leaf] = part
    for c in scatter:
        c.wait_send()
    for c in gather:
        c.wait()
    for p in range(n_leaf):
        at, wide = (p * rows) % m, (p * rows) // m * LANES
        yt_ref[at : at + rows, wide : wide + LANES] = yall[p]


def project_kernel(x_hbm, yt_ref, o_hbm, xbuf, obuf, phi, pmid, rows_ref, sems, osems):
    chunks = x_hbm.shape[0] // CHUNK

    def copy(i):
        at = pl.ds(pl.multiple_of(i * CHUNK, CHUNK), CHUNK)
        return pltpu.make_async_copy(x_hbm.at[at], xbuf.at[at], sems.at[i])

    def out(i):
        at = pl.ds(pl.multiple_of(i * CHUNK, CHUNK), CHUNK)
        return pltpu.make_async_copy(obuf.at[at], o_hbm.at[at], osems.at[i])

    for i in range(chunks):
        copy(i).start()
    qt = orthonormal(yt_ref[...], rows_ref)
    hi, mid = split(dot(qt, qt, 0, 0))
    phi[...] = hi
    pmid[...] = mid

    def step(i, carry):
        copy(i).wait()
        at = pl.ds(pl.multiple_of(i * CHUNK, CHUNK), CHUNK)
        hi, mid = split(xbuf[at, :])
        obuf[at, :] = (fast(hi, phi[...]) + (fast(hi, pmid[...]) + fast(mid, phi[...]))).astype(jnp.bfloat16)
        out(i).start()
        return carry

    lax.fori_loop(0, chunks, step, 0)
    for i in range(chunks):
        out(i).wait()


def local(n_grp, n_leaf, x, sketch):
    rows, cols = x.shape
    modes = sketch.shape[1]
    chunks = rows // CHUNK
    f32 = jnp.float32
    hbm = pl.BlockSpec(memory_space=pl.ANY)
    dma = pltpu.SemaphoreType.DMA
    piece = (modes * cols // (n_leaf * LANES), LANES)
    yt = pl.pallas_call(
        functools.partial(merge_kernel, n_grp, n_leaf),
        out_shape=jax.ShapeDtypeStruct((modes, cols), f32),
        in_specs=[hbm, VMEM],
        out_specs=VMEM,
        scratch_shapes=[
            pltpu.VMEM((rows, cols), f32), pltpu.VMEM((cols, 2 * cols), f32), pltpu.VMEM((cols, cols), f32),
            pltpu.VMEM((modes, 2 * modes), f32),
            pltpu.VMEM((n_grp, modes, cols), f32), pltpu.VMEM((n_grp, modes, modes), f32),
            pltpu.VMEM((n_leaf, *piece), f32), pltpu.VMEM((n_leaf - 1, *piece), f32),
            pltpu.VMEM(piece, f32), pltpu.VMEM((n_leaf, *piece), f32),
            dma((chunks,)), dma((2, n_grp - 1)), dma((2, n_grp - 1)), dma((2, n_leaf - 1)), dma((2, n_leaf - 1)),
        ],
        compiler_params=pltpu.CompilerParams(collective_id=0, has_side_effects=True),
    )(x, sketch.T)
    return pl.pallas_call(
        project_kernel,
        out_shape=jax.ShapeDtypeStruct((rows, cols), jnp.bfloat16),
        in_specs=[hbm, VMEM],
        out_specs=hbm,
        scratch_shapes=[
            pltpu.VMEM((rows, cols), f32), pltpu.VMEM((rows, cols), jnp.bfloat16),
            pltpu.VMEM((cols, cols), jnp.bfloat16), pltpu.VMEM((cols, cols), jnp.bfloat16),
            pltpu.VMEM((modes, 2 * modes), f32), dma((chunks,)), dma((chunks,)),
        ],
    )(x, yt)


def solution(mesh):
    return jax.shard_map(
        functools.partial(local, mesh.shape["grp"], mesh.shape["leaf"]),
        mesh=mesh,
        in_specs=(P(("grp", "leaf"), None), P()),
        out_specs=P(("grp", "leaf"), None),
        check_vma=False,
    )
```

time: 53.5 us -> 40.9 us (0.76)
  Pallas kernels: 50.2 us -> 40.7 us
  local copies, waits for them, and re-layouts: 1.56 us -> 0 us
  other arithmetic: 1.25 us -> 0 us
    pallas_call x4 -> x1, Pallas kernels: 41 us -> 31.6 us  [local(): pl.pallas_call(functools.partial(merge_kernel, n_grp, n_leaf), out_shape=...]
    slice x2 -> x0, local copies, waits for them, and re-layouts: 1.56 us -> none  [the longest x1 0.78 us: local(): y[modes * i:modes * i + modes]]
    reshape x1 -> x0, other arithmetic: 0.63 us -> none  [local(): jnp.concatenate([zt[:, LANES * i:LANES * i + LANES] for i in range(wide)]...]
    concatenate x1 -> x0, other arithmetic: 0.62 us -> none  [local(): jnp.concatenate([y[modes * i:modes * i + modes] for i in range(wide)], ax...]
where the time goes in v2:
time: 40.9 us; the launch traced here: 40.7 us
  Pallas kernels  40.7 us (100%)
    pallas_call x1, Pallas kernels, local(): pl.pallas_call(functools.partial(merge_kernel, n_grp, n_leaf), out_shape=...  31.6 us
    pallas_call x1, Pallas kernels, local(): pl.pallas_call(project_kernel, out_shape=jax.ShapeDtypeStruct((rows, cols...  9.06 us

profile of v2, /device:TPU:0, one launch (start us, length us, event | category | flops | bytes accessed | tf_op | source)
XLA Modules:
  0.0 40.7 jit_solution(18238415076545240603)
XLA Ops:
  0.0 31.6 %shard_map.28.yt_ref = f32[64,256]{1,0:T(8,128)} custom-call(f32[4096,256]{1,0:T(8,128)} %x_hbm.3, f32[64,256]{1,0:T(8,128)} %bitcast.1), custom_call_target="tpu_custom_call" | custom-call | tf_op jit(solution)/shard_map/pallas_call | solution.py:205
  31.6 9.1 %shard_map.29 = bf16[4096,256]{1,0:T(8,128)(2,1)} custom-call(f32[4096,256]{1,0:T(8,128)} %x_hbm.3, f32[64,256]{1,0:T(8,128)} %shard_map.28.yt_ref), custom_call_target="tpu_custom_call" | custom-call | tf_op jit(solution)/shard_map/pallas_call | solution.py:220

commit v3 on v2

--- a/solution.py
+++ b/solution.py
@@ -38,33 +38,59 @@
     return (lax.broadcasted_iota(jnp.int32, (n, n), 0) == lax.broadcasted_iota(jnp.int32, (n, n), 1)).astype(jnp.float32)
 
 
-def inverse_factor(c, rows_ref):
+def eliminate(s, rhs, emit):
+    b = len(s)
+    if b == 2:
+        det = s[0][0] * s[1][1] - s[1][0] * s[1][0]
+        inv = 1.0 / det
+        low = [s[0][0] * r[1] - s[1][0] * r[0] for r in rhs]
+        if emit is not None:
+            scale = lax.rsqrt(s[0][0])
+            emit(rhs[0][0] * scale)
+            emit(low[0] * (scale * lax.rsqrt(det)))
+        return [[(s[1][1] * r[0] - s[1][0] * r[1]) * inv, l * inv] for r, l in zip(rhs, low)]
+    h = b // 2
+    side = [[s[h + p][q] for q in range(h)] for p in range(h)]
+    upper = [[s[p][q] if q <= p else s[q][p] for q in range(h)] for p in range(h)]
+    done = eliminate(upper, [r[:h] for r in rhs] + side, emit)
+    tops, u = done[: len(rhs)], done[len(rhs) :]
+
+    def apply(row, vector):
+        terms = [row[q] * vector[q] for q in range(h)]
+        while len(terms) > 1:
+            terms = [x + y for x, y in zip(terms[::2], terms[1::2])]
+        return terms[0]
+
+    schur = [[s[h + p][h + q] - apply(side[p], u[q]) if q <= p else None for q in range(h)] for p in range(h)]
+    rest = [[r[h + p] - apply(side[p], t) for p in range(h)] for r, t in zip(rhs, tops)]
+    bottoms = eliminate(schur, rest, emit)
+    return [
+        [t[p] - apply([u[q][p] for q in range(h)], v) for p in range(h)] + v for t, v in zip(tops, bottoms)
+    ]
+
+
+def inverse_factor(c, rows_ref, b=8):
     m = c.shape[0]
     full = jnp.concatenate([c, identity(m)], axis=1)
-    width = 2 * m
+    tile = (8, 2 * m)
     blocks = [full[8 * k : 8 * k + 8] for k in range(m // 8)]
-    for j in range(0, m, 2):
-        k, s = j // 8, j % 8
-        lead = blocks[k]
-        cols = [
-            (
-                jnp.broadcast_to(blocks[i][:, j : j + 1], (8, width)),
-                jnp.broadcast_to(blocks[i][:, j + 1 : j + 2], (8, width)),
-            )
-            for i in range(k, m // 8)
-        ]
-        r0, r1 = lead[s : s + 1], lead[s + 1 : s + 2]
-        a, b, d = cols[0][0][s : s + 1], cols[0][0][s + 1 : s + 2], cols[0][1][s + 1 : s + 2]
-        det = a * d - b * b
-        inv = 1.0 / det
-        t0 = (d * r0 - b * r1) * inv
-        t1 = (a * r1 - b * r0) * inv
-        for i in range(k, m // 8):
-            c0, c1 = cols[i - k]
-            blocks[i] = blocks[i] - c0 * t0 - c1 * t1
-        ia = lax.rsqrt(a)
-        rows_ref[j : j + 1, :] = r0 * ia
-        rows_ref[j + 1 : j + 2, :] = (a * r1 - b * r0) * (ia * lax.rsqrt(det))
+    for j in range(0, m, b):
+        k, at = j // 8, j % 8
+        cols = [[jnp.broadcast_to(blocks[i][:, j + q : j + q + 1], tile) for q in range(b)] for i in range(k, m // 8)]
+        rows = [jnp.broadcast_to(blocks[k][at + p : at + p + 1], tile) for p in range(b)]
+        pivot = [[jnp.broadcast_to(cols[0][q][at + p : at + p + 1], tile) if q <= p else None for q in range(b)] for p in range(b)]
+        place = [j]
+
+        def emit(row):
+            rows_ref[place[0] : place[0] + 1, :] = row[:1]
+            place[0] += 1
+
+        (t,) = eliminate(pivot, [rows], emit)
+        for i in range(k if at + b < 8 else k + 1, m // 8):
+            terms = [x * y for x, y in zip(cols[i - k], t)]
+            while len(terms) > 1:
+                terms = [x + y for x, y in zip(terms[::2], terms[1::2])]
+            blocks[i] = blocks[i] - terms[0]
     return rows_ref[:, m:]
 
 
@@ -127,16 +153,13 @@
         c.wait()
     st = st_ref[...]
     qs = qall[...].reshape(n_grp * m, cols)
-    us = dot(st, qs, 1, 1)
     for c in to_group_h:
         c.wait()
-    vs = jnp.concatenate([dot(us[:, g * m : g * m + m], hall[g]) for g in range(n_grp)], axis=1)
-    q2 = orthonormal(dot(vs, qs), rows_ref)
-    u = dot(st, q2, 1, 1)
-    s = dot(q2, qs, 1, 1)
-    w = dot(u, s)
-    w = jnp.concatenate([dot(w[:, g * m : g * m + m], hall[g]) for g in range(n_grp)], axis=1)
-    zt = dot(dot(w, s, 1, 1), q2)
+    ts = jnp.concatenate([dot(hall[g], qs[g * m : g * m + m]) for g in range(n_grp)], axis=0)
+    pair_gram = dot(qs, ts, 0, 0)
+    q2 = orthonormal(dot(st, pair_gram), rows_ref)
+    h2 = dot(dot(q2, pair_gram), q2, 1, 1)
+    zt = dot(dot(dot(st, q2, 1, 1), h2), q2)
 
     rows = z.shape[1]
     for p in range(n_leaf):
@@ -163,7 +186,7 @@
         yt_ref[at : at + rows, wide : wide + LANES] = yall[p]
 
 
-def project_kernel(x_hbm, yt_ref, o_hbm, xbuf, obuf, phi, pmid, rows_ref, sems, osems):
+def project_kernel(x_hbm, yt_ref, o_hbm, xbuf, obuf, proj, rows_ref, sems, osems):
     chunks = x_hbm.shape[0] // CHUNK
 
     def copy(i):
@@ -178,14 +201,13 @@
         copy(i).start()
     qt = orthonormal(yt_ref[...], rows_ref)
     hi, mid = split(dot(qt, qt, 0, 0))
-    phi[...] = hi
-    pmid[...] = mid
+    proj[...] = jnp.concatenate([hi, mid, hi], axis=0)
 
     def step(i, carry):
         copy(i).wait()
         at = pl.ds(pl.multiple_of(i * CHUNK, CHUNK), CHUNK)
         hi, mid = split(xbuf[at, :])
-        obuf[at, :] = (fast(hi, phi[...]) + (fast(hi, pmid[...]) + fast(mid, phi[...]))).astype(jnp.bfloat16)
+        obuf[at, :] = fast(jnp.concatenate([hi, hi, mid], axis=1), proj[...]).astype(jnp.bfloat16)
         out(i).start()
         return carry
 
@@ -224,7 +246,7 @@
         out_specs=hbm,
         scratch_shapes=[
             pltpu.VMEM((rows, cols), f32), pltpu.VMEM((rows, cols), jnp.bfloat16),
-            pltpu.VMEM((cols, cols), jnp.bfloat16), pltpu.VMEM((cols, cols), jnp.bfloat16),
+            pltpu.VMEM((3 * cols, cols), jnp.bfloat16),
             pltpu.VMEM((modes, 2 * modes), f32), dma((chunks,)), dma((chunks,)),
         ],
     )(x, yt)

time: 40.9 us -> 38.6 us (0.944)
  Pallas kernels: 40.7 us -> 38.4 us
    pallas_call x1, Pallas kernels: 31.6 us -> 30.2 us  [local(): pl.pallas_call(functools.partial(merge_kernel, n_grp, n_leaf), out_shape=...]
    pallas_call x1, Pallas kernels: 9.06 us -> 8.18 us  [local(): pl.pallas_call(project_kernel, out_shape=jax.ShapeDtypeStruct((rows, cols...]
where the time goes in v3:
time: 38.6 us; the launch traced here: 38.4 us
  Pallas kernels  38.4 us (99%)
    pallas_call x1, Pallas kernels, local(): pl.pallas_call(functools.partial(merge_kernel, n_grp, n_leaf), out_shape=...  30.2 us
    pallas_call x1, Pallas kernels, local(): pl.pallas_call(project_kernel, out_shape=jax.ShapeDtypeStruct((rows, cols...  8.18 us

profile of v3, /device:TPU:0, one launch (start us, length us, event | category | flops | bytes accessed | tf_op | source)
XLA Modules:
  0.0 38.4 jit_solution(8544816709891671510)
XLA Ops:
  0.0 30.2 %shard_map.28.yt_ref = f32[64,256]{1,0:T(8,128)} custom-call(f32[4096,256]{1,0:T(8,128)} %x_hbm.3, f32[64,256]{1,0:T(8,128)} %bitcast.1), custom_call_target="tpu_custom_call" | custom-call | tf_op jit(solution)/shard_map/pallas_call | solution.py:227
  30.3 8.2 %shard_map.29 = bf16[4096,256]{1,0:T(8,128)(2,1)} custom-call(f32[4096,256]{1,0:T(8,128)} %x_hbm.3, f32[64,256]{1,0:T(8,128)} %shard_map.28.yt_ref), custom_call_target="tpu_custom_call" | custom-call | tf_op jit(solution)/shard_map/pallas_call | solution.py:242

commit v4 on v3

--- a/solution.py
+++ b/solution.py
@@ -10,7 +10,7 @@
 MESH = pl.DeviceIdType.MESH
 VMEM = pl.BlockSpec(memory_space=pltpu.VMEM)
 LANES = 128
-CHUNK = 512
+CHUNK = 1024
 
 
 def dot(a, b, ca=1, cb=0):

time: 38.6 us -> 37.3 us (0.966)
  Pallas kernels: 38.4 us -> 37.1 us
    pallas_call x1, Pallas kernels: 30.2 us -> 29.5 us  [local(): pl.pallas_call(functools.partial(merge_kernel, n_grp, n_leaf), out_shape=...]
    pallas_call x1, Pallas kernels: 8.18 us -> 7.52 us  [local(): pl.pallas_call(project_kernel, out_shape=jax.ShapeDtypeStruct((rows, cols...]
where the time goes in v4:
time: 37.3 us; the launch traced here: 37.1 us
  Pallas kernels  37.1 us (99%)
    pallas_call x1, Pallas kernels, local(): pl.pallas_call(functools.partial(merge_kernel, n_grp, n_leaf), out_shape=...  29.5 us
    pallas_call x1, Pallas kernels, local(): pl.pallas_call(project_kernel, out_shape=jax.ShapeDtypeStruct((rows, cols...  7.52 us

profile of v4, /device:TPU:0, one launch (start us, length us, event | category | flops | bytes accessed | tf_op | source)
XLA Modules:
  0.0 37.1 jit_solution(3632686181054127520)
XLA Ops:
  0.0 29.5 %shard_map.28.yt_ref = f32[64,256]{1,0:T(8,128)} custom-call(f32[4096,256]{1,0:T(8,128)} %x_hbm.3, f32[64,256]{1,0:T(8,128)} %bitcast.1), custom_call_target="tpu_custom_call" | custom-call | tf_op jit(solution)/shard_map/pallas_call | solution.py:227
  29.5 7.5 %shard_map.29 = bf16[4096,256]{1,0:T(8,128)(2,1)} custom-call(f32[4096,256]{1,0:T(8,128)} %x_hbm.3, f32[64,256]{1,0:T(8,128)} %shard_map.28.yt_ref), custom_call_target="tpu_custom_call" | custom-call | tf_op jit(solution)/shard_map/pallas_call | solution.py:242
